TPU v7x, 32 devices: a whole 2x2x4 slice. The times are simulated.
32 devices in a mesh: parts: 2 (over y), rows: 4 (over x, core), cols: 4 (over z).
Axes of the slice: x: 2, y: 2, z: 4, core: 2. Of those that a mesh axis runs over, the one named last changes fastest.
Arguments:
- singles: bfloat16 [1024, 384], P(('parts', 'rows', 'cols')), parts along dimension 0, may hold values from -120 to 120
- pair: bfloat16 [1024, 512, 128], P(('parts', 'rows'), 'cols'), parts along dimension 0, may hold values from -6 to 6
- chain_sizes: int32 [16], P('parts'), parts along dimension 0, may hold values from 1 to 128, 512 in all
- single_proj: bfloat16 [384, 1536], replicated, may hold values from -1 to 1
- query_bias: float32 [384], replicated, may hold values from -5 to 5
- pair_proj: bfloat16 [128, 16], replicated, may hold values from -0.5 to 0.5
- out_proj: bfloat16 [384, 384], replicated, may hold values from -1.25 to 1.25
Outputs:
- update: bfloat16 [1024, 384], P(('parts', 'rows', 'cols')), parts along dimension 0
There are 2 independent parts, one for each index of `parts`. A program takes and returns all parts, laid end to end along the dimension named above; an argument that names none is the same for every part. Nothing has to cross between parts.
Inputs may be any that keep to these rules, and one draw needn't show every extreme that they name: `chain_sizes`: the first 7 entries count the tokens of the chains in order; the last one counts the padding tokens at the end of the complex.
All inputs are finite; a program needn't handle non-finite values.
Results may differ from a plain program's by a relative error of at most 0.004.
The roundings to bfloat16 on the way count: a program that leaves them out, or rounds other values in their place, can miss the bound.
Values may be sent and summed in bfloat16 or wider, within the bound.
A program may use at most 64 MiB of HBM per device.

v0:
```python
import math
import jax
import jax.numpy as jnp
from jax import lax
from jax.sharding import PartitionSpec as P


def normalize(matrix):
    average = jnp.mean(matrix, axis=-1, keepdims=True)
    centered = matrix - average
    variance = jnp.mean(centered * centered, axis=-1, keepdims=True)
    return centered * lax.rsqrt(variance + 1e-05)


def tile_bias(pair, pair_proj):
    tile_rows, tile_cols, channels = pair.shape
    head_count = pair_proj.shape[1]
    row_block = math.gcd(tile_rows, 32)
    blocks = pair.reshape(tile_rows // row_block, row_block, tile_cols, channels)

    def project(pair_rows):
        pair_normed = normalize(pair_rows.astype(jnp.float32)).astype(jnp.bfloat16)
        return jnp.einsum(
            "ikc,ch->hik", pair_normed, pair_proj, preferred_element_type=jnp.float32
        ).astype(jnp.bfloat16)

    stacked = lax.map(project, blocks)
    return jnp.moveaxis(stacked, 1, 0).reshape(head_count, tile_rows, tile_cols)


def shards(singles, pair, chain_sizes, single_proj, query_bias, pair_proj, out_proj):
    own_rows, features = singles.shape
    head_count = pair_proj.shape[1]
    head_dim = features // head_count
    score_scale = head_dim ** (-0.5)
    normed = normalize(singles.astype(jnp.float32)).astype(jnp.bfloat16)
    projected = jnp.dot(normed, single_proj, preferred_element_type=jnp.float32)
    queries = (projected[:, :features] + query_bias).astype(jnp.bfloat16)
    key_rows = projected[:, features : 2 * features].astype(jnp.bfloat16)
    values = projected[:, 2 * features : 3 * features].astype(jnp.bfloat16)
    gating = jax.nn.sigmoid(projected[:, 3 * features :])
    live_count = jnp.sum(chain_sizes[:-1])
    bias_tile = tile_bias(pair, pair_proj)
    key_value = jnp.concatenate([key_rows, values], axis=1)
    gathered = lax.all_gather(key_value, ("rows", "cols"), axis=0, tiled=True)
    bias_own = lax.all_to_all(bias_tile, "cols", split_axis=1, concat_axis=2, tiled=True)
    key_count = gathered.shape[0]
    key_heads = gathered[:, :features].reshape(key_count, head_count, head_dim)
    value_heads = gathered[:, features:].reshape(key_count, head_count, head_dim)
    query_heads = queries.reshape(own_rows, head_count, head_dim)
    scores = jnp.einsum(
        "qhd,khd->hqk", query_heads, key_heads, preferred_element_type=jnp.float32
    ) * score_scale + bias_own.astype(jnp.float32)
    key_live = jnp.arange(key_count, dtype=jnp.int32) < live_count
    scores = jnp.where(key_live[None, None, :], scores, -1e30)
    maxima = jnp.max(scores, axis=-1, keepdims=True)
    weights = jnp.exp(scores - maxima)
    totals = jnp.sum(weights, axis=-1)
    numerator = jnp.einsum(
        "hqk,khd->qhd",
        weights.astype(jnp.bfloat16),
        value_heads,
        preferred_element_type=jnp.float32,
    )
    averaged = (numerator / jnp.transpose(totals)[:, :, None]).reshape(own_rows, features)
    attended = (gating * averaged).astype(jnp.bfloat16)
    return jnp.dot(attended, out_proj, preferred_element_type=jnp.float32).astype(jnp.bfloat16)


def solution(mesh):
    placed = (
        P(("parts", "rows", "cols"), None),
        P(("parts", "rows"), "cols", None),
        P("parts"),
        P(),
        P(),
        P(),
        P(),
    )
    return jax.shard_map(
        shards,
        mesh=mesh,
        in_specs=placed,
        out_specs=P(("parts", "rows", "cols"), None),
        check_vma=False,
    )
```

profile of v0, /device:TPU:0, one launch (start us, length us, event | category | flops | bytes accessed | tf_op | source)
XLA Modules:
  0.0 86.1 jit_solution(3081833499026486826)
XLA Ops:
  0.0 0.0 copy-start
  0.0 0.0 copy-start.2
  0.0 28.6 %while.10 = (s32[]{:T(128)}, bf16[4,16,32,128]{3,1,2,0:T(8,128)(2,1)}, bf16[4,32,128,128]{3,2,1,0:T(8,128)(2,1)}, bf16[128,16]{0,1:T(8,128)(2,1)}, s32[]{:T(128)}) while((s32[]{:T(128)}, bf16[4,16,32,128]{3,1,2,0:T(8,128)(2,1)}, bf16[4,32,128,128]{3,2,1,0:T(8,128)(2,1)}, bf16[128,16]{0,1:T(8,128)(2,1)}, s32[]{:T(128)}) %tuple.23), condition=%wide.region_6.7_spmd, body=%wide.region_3.6_spmd.sunk | while | flops 22089728 | bytes 3445865 | solution.py:27
  0.0 0.0 copy-start.4
  0.0 1.7 %convert_reduce_fusion.3 = f32[32,128]{1,0:T(8,128)S(1)} fusion(bf16[4,32,128,128]{3,2,1,0:T(8,128)(2,1)} %get-tuple-element.77, s32[]{:T(128)S(6)} %copy.31), kind=kLoop, calls=%fused_computation.clone.1 | loop fusion | flops 1044480 | bytes 1064964 | tf_op jit(solution)/shard_map/while/body/eval_jaxpr/reduce_sum | solution.py:9
  1.7 2.3 %fusion.50 = f32[32,128]{1,0:T(8,128)S(1)} fusion(f32[32,128]{1,0:T(8,128)S(1)} %broadcast_multiply_fusion.3, bf16[4,32,128,128]{3,2,1,0:T(8,128)(2,1)} %get-tuple-element.77, s32[]{:T(128)S(6)} %copy.31), kind=kLoop, calls=%fused_computation.5.clone.1 | loop fusion | flops 2093056 | bytes 1081348 | tf_op jit(solution)/shard_map/while/body/eval_jaxpr/reduce_sum | solution.py:11
  4.1 0.0 copy-done.4
  4.1 3.1 %fusion.51 = bf16[4,16,32,128]{3,1,2,0:T(8,128)(2,1)} fusion(bf16[4,16,32,128]{3,1,2,0:T(8,128)(2,1)} %get-tuple-element.71, s32[]{:T(128)S(6)} %copy.31, f32[32,128]{1,0:T(8,128)S(1)} %add_rsqrt_fusion.3, f32[32,128]{1,0:T(8,128)S(1)} %broadcast_multiply_fusion.3, bf16[4,32,128,128]{3,2,1,0:T(8,128)(2,1)} %get-tuple-element.77, ...), kind=kOutput, calls=%fused_computation.9.clone.1 | convolution fusion | flops 18939904 | bytes 1217536 | tf_op jit(solution)/shard_map/while/body/eval_jaxpr/ikc,ch->hik/dot_general | solution.py:23
  7.2 0.0 copy-start.4
  7.2 1.6 %convert_reduce_fusion.3 = f32[32,128]{1,0:T(8,128)S(1)} fusion(bf16[4,32,128,128]{3,2,1,0:T(8,128)(2,1)} %get-tuple-element.77, s32[]{:T(128)S(6)} %copy.31), kind=kLoop, calls=%fused_computation.clone.1 | loop fusion | flops 1044480 | bytes 1064964 | tf_op jit(solution)/shard_map/while/body/eval_jaxpr/reduce_sum | solution.py:9
  8.8 2.3 %fusion.50 = f32[32,128]{1,0:T(8,128)S(1)} fusion(f32[32,128]{1,0:T(8,128)S(1)} %broadcast_multiply_fusion.3, bf16[4,32,128,128]{3,2,1,0:T(8,128)(2,1)} %get-tuple-element.77, s32[]{:T(128)S(6)} %copy.31), kind=kLoop, calls=%fused_computation.5.clone.1 | loop fusion | flops 2093056 | bytes 1081348 | tf_op jit(solution)/shard_map/while/body/eval_jaxpr/reduce_sum | solution.py:11
  11.2 0.0 copy-done.4
  11.2 3.2 %fusion.51 = bf16[4,16,32,128]{3,1,2,0:T(8,128)(2,1)} fusion(bf16[4,16,32,128]{3,1,2,0:T(8,128)(2,1)} %get-tuple-element.71, s32[]{:T(128)S(6)} %copy.31, f32[32,128]{1,0:T(8,128)S(1)} %add_rsqrt_fusion.3, f32[32,128]{1,0:T(8,128)S(1)} %broadcast_multiply_fusion.3, bf16[4,32,128,128]{3,2,1,0:T(8,128)(2,1)} %get-tuple-element.77, ...), kind=kOutput, calls=%fused_computation.9.clone.1 | convolution fusion | flops 18939904 | bytes 1217536 | tf_op jit(solution)/shard_map/while/body/eval_jaxpr/ikc,ch->hik/dot_general | solution.py:23
  14.4 0.0 copy-start.4
  14.4 1.6 %convert_reduce_fusion.3 = f32[32,128]{1,0:T(8,128)S(1)} fusion(bf16[4,32,128,128]{3,2,1,0:T(8,128)(2,1)} %get-tuple-element.77, s32[]{:T(128)S(6)} %copy.31), kind=kLoop, calls=%fused_computation.clone.1 | loop fusion | flops 1044480 | bytes 1064964 | tf_op jit(solution)/shard_map/while/body/eval_jaxpr/reduce_sum | solution.py:9
  16.0 2.3 %fusion.50 = f32[32,128]{1,0:T(8,128)S(1)} fusion(f32[32,128]{1,0:T(8,128)S(1)} %broadcast_multiply_fusion.3, bf16[4,32,128,128]{3,2,1,0:T(8,128)(2,1)} %get-tuple-element.77, s32[]{:T(128)S(6)} %copy.31), kind=kLoop, calls=%fused_computation.5.clone.1 | loop fusion | flops 2093056 | bytes 1081348 | tf_op jit(solution)/shard_map/while/body/eval_jaxpr/reduce_sum | solution.py:11
  18.3 0.0 copy-done.4
  18.3 3.2 %fusion.51 = bf16[4,16,32,128]{3,1,2,0:T(8,128)(2,1)} fusion(bf16[4,16,32,128]{3,1,2,0:T(8,128)(2,1)} %get-tuple-element.71, s32[]{:T(128)S(6)} %copy.31, f32[32,128]{1,0:T(8,128)S(1)} %add_rsqrt_fusion.3, f32[32,128]{1,0:T(8,128)S(1)} %broadcast_multiply_fusion.3, bf16[4,32,128,128]{3,2,1,0:T(8,128)(2,1)} %get-tuple-element.77, ...), kind=kOutput, calls=%fused_computation.9.clone.1 | convolution fusion | flops 18939904 | bytes 1217536 | tf_op jit(solution)/shard_map/while/body/eval_jaxpr/ikc,ch->hik/dot_general | solution.py:23
  21.5 0.0 copy-start.4
  21.5 1.6 %convert_reduce_fusion.3 = f32[32,128]{1,0:T(8,128)S(1)} fusion(bf16[4,32,128,128]{3,2,1,0:T(8,128)(2,1)} %get-tuple-element.77, s32[]{:T(128)S(6)} %copy.31), kind=kLoop, calls=%fused_computation.clone.1 | loop fusion | flops 1044480 | bytes 1064964 | tf_op jit(solution)/shard_map/while/body/eval_jaxpr/reduce_sum | solution.py:9
  23.1 2.3 %fusion.50 = f32[32,128]{1,0:T(8,128)S(1)} fusion(f32[32,128]{1,0:T(8,128)S(1)} %broadcast_multiply_fusion.3, bf16[4,32,128,128]{3,2,1,0:T(8,128)(2,1)} %get-tuple-element.77, s32[]{:T(128)S(6)} %copy.31), kind=kLoop, calls=%fused_computation.5.clone.1 | loop fusion | flops 2093056 | bytes 1081348 | tf_op jit(solution)/shard_map/while/body/eval_jaxpr/reduce_sum | solution.py:11
  25.4 0.0 copy-done.4
  25.5 3.2 %fusion.51 = bf16[4,16,32,128]{3,1,2,0:T(8,128)(2,1)} fusion(bf16[4,16,32,128]{3,1,2,0:T(8,128)(2,1)} %get-tuple-element.71, s32[]{:T(128)S(6)} %copy.31, f32[32,128]{1,0:T(8,128)S(1)} %add_rsqrt_fusion.3, f32[32,128]{1,0:T(8,128)S(1)} %broadcast_multiply_fusion.3, bf16[4,32,128,128]{3,2,1,0:T(8,128)(2,1)} %get-tuple-element.77, ...), kind=kOutput, calls=%fused_computation.9.clone.1 | convolution fusion | flops 18939904 | bytes 1217536 | tf_op jit(solution)/shard_map/while/body/eval_jaxpr/ikc,ch->hik/dot_general | solution.py:23
  28.6 6.5 %all-to-all-start = ((bf16[16,128,128]{2,0,1:T(8,128)(2,1)}), bf16[16,128,128]{2,0,1:T(8,128)(2,1)S(1)}, u32[]{:S(2)}, u32[]{:S(2)}) async-start(bf16[16,128,128]{2,0,1:T(8,128)(2,1)} %bitcast.9), calls=%async_computation | async-start | bytes 1048576 | tf_op jit(solution)/shard_map/all_to_all | solution.py:46
  35.1 0.0 copy-done.2
  35.1 0.1 convert_reduce_fusion.1
  35.2 0.2 fusion.22
  35.4 0.0 copy-done
  35.4 0.4 fusion.31
  35.8 0.0 copy-done.3
  35.8 0.0 copy-start.5
  35.8 0.1 copy.24
  36.0 46.1 %all_gather.3 = bf16[512,768]{1,0:T(8,128)(2,1)S(1)} all-gather(bf16[32,768]{1,0:T(8,128)(2,1)S(1)} %slice.53), channel_id=1, replica_groups=mesh['parts'=2,'rows'=4,'cols'=4] {'rows','cols'}, dimensions={0}, use_global_device_ids=true | all-gather | bytes 835584 | tf_op jit(solution)/shard_map/all_gather | solution.py:45
  82.1 0.1 fusion.37
  82.2 0.2 copy.19
  82.4 0.2 copy.18
  82.6 0.0 copy-done.5
  82.6 0.6 slice_reduce_fusion
  83.2 0.6 iota_compare_fusion
  83.9 0.0 all-to-all-done
  83.9 0.1 copy.21
  84.0 0.0 copy-start.1
  84.0 0.5 fusion.38
  84.5 0.3 fusion.16
  84.8 0.3 fusion.15
  85.2 0.1 copy.25
  85.3 0.0 copy-done.1
  85.3 0.8 convolution_convert_fusion.1
  (14 shorter events, 0.1 us)
Async XLA Ops:
  0.0 35.4 %copy-start = (bf16[384,1536]{1,0:T(8,128)(2,1)S(1)}, bf16[384,1536]{1,0:T(8,128)(2,1)}, u32[]{:S(2)}) copy-start(bf16[384,1536]{1,0:T(8,128)(2,1)} %param.12) | copy-start | bytes 3538948
  0.0 35.1 %copy-start.2 = (bf16[32,384]{1,0:T(8,128)(2,1)S(1)}, bf16[32,384]{1,0:T(8,128)(2,1)}, u32[]{:S(2)}) copy-start(bf16[32,384]{1,0:T(8,128)(2,1)} %param.9) | copy-start | bytes 73732
  0.0 4.1 %copy-start.4 = (bf16[128,16]{0,1:T(8,128)(2,1)S(1)}, bf16[128,16]{0,1:T(8,128)(2,1)}, u32[]{:S(2)}) copy-start(bf16[128,16]{0,1:T(8,128)(2,1)} %get-tuple-element.78) | copy-start | bytes 12292 | tf_op jit(solution)/shard_map/while
  7.2 4.0 %copy-start.4 = (bf16[128,16]{0,1:T(8,128)(2,1)S(1)}, bf16[128,16]{0,1:T(8,128)(2,1)}, u32[]{:S(2)}) copy-start(bf16[128,16]{0,1:T(8,128)(2,1)} %get-tuple-element.78) | copy-start | bytes 12292 | tf_op jit(solution)/shard_map/while
  14.4 4.0 %copy-start.4 = (bf16[128,16]{0,1:T(8,128)(2,1)S(1)}, bf16[128,16]{0,1:T(8,128)(2,1)}, u32[]{:S(2)}) copy-start(bf16[128,16]{0,1:T(8,128)(2,1)} %get-tuple-element.78) | copy-start | bytes 12292 | tf_op jit(solution)/shard_map/while
  21.5 4.0 %copy-start.4 = (bf16[128,16]{0,1:T(8,128)(2,1)S(1)}, bf16[128,16]{0,1:T(8,128)(2,1)}, u32[]{:S(2)}) copy-start(bf16[128,16]{0,1:T(8,128)(2,1)} %get-tuple-element.78) | copy-start | bytes 12292 | tf_op jit(solution)/shard_map/while
  28.6 7.2 %copy-start.3 = (f32[384]{0:T(512)S(1)}, f32[384]{0:T(512)}, u32[]{:S(2)}) copy-start(f32[384]{0:T(512)} %param.13) | copy-start | bytes 4612
  28.6 55.3 %all-to-all-start = ((bf16[16,128,128]{2,0,1:T(8,128)(2,1)}), bf16[16,128,128]{2,0,1:T(8,128)(2,1)S(1)}, u32[]{:S(2)}, u32[]{:S(2)}) async-start(bf16[16,128,128]{2,0,1:T(8,128)(2,1)} %bitcast.9), calls=%async_computation | async-start | bytes 1048576 | tf_op jit(solution)/shard_map/all_to_all | solution.py:46
  35.8 46.8 %copy-start.5 = (s32[8]{0:T(128)S(1)}, s32[8]{0:T(128)}, u32[]{:S(2)}) copy-start(s32[8]{0:T(128)} %param.11) | copy-start | bytes 100
  84.0 1.3 %copy-start.1 = (bf16[384,384]{1,0:T(8,128)(2,1)S(1)}, bf16[384,384]{1,0:T(8,128)(2,1)}, u32[]{:S(2)}) copy-start(bf16[384,384]{1,0:T(8,128)(2,1)} %param.15) | copy-start | bytes 884740
where the time goes:
time: 86.6 us; the launch traced here: 86.1 us
  blocking collectives  46.1 us (53%)
  other arithmetic  17.8 us (21%)
  matrix products  14.6 us (17%)
  starting transfers between devices  6.48 us (7%)
  local copies, waits for them, and re-layouts  0.87 us (1%)
    all_gather x1, blocking collectives, shards(): gathered = lax.all_gather(key_value, ('rows', 'cols'), axis=0, tiled=True)  46.1 us
    dot_general x4, matrix products, project(): jnp.einsum('ikc,ch->hik', pair_normed, pair_proj, preferred_element_type=...  12.6 us
    reduce_sum x5, other arithmetic, normalize(): variance = jnp.mean(centered * centered, axis=-1, keepdims=True)  9.52 us
    reduce_sum x5, other arithmetic, normalize(): average = jnp.mean(matrix, axis=-1, keepdims=True)  6.56 us
    all_to_all x1, starting transfers between devices, shards(): lax.all_to_all(bias_tile, 'cols', split_axis=1, concat_axis=2, tiled=True)  6.48 us
  transfers between devices with their start and end apart: 1, of which 0 were waited for; matrix products, arithmetic and copies ran while one was open for 3% of the time, Pallas kernels for 0%

commit v1 on v0

--- a/solution.py
+++ b/solution.py
@@ -1,8 +1,32 @@
+import functools
 import math
 import jax
 import jax.numpy as jnp
 from jax import lax
 from jax.sharding import PartitionSpec as P
+
+
+def draft_tails(block_here, along_dim, k_dim):
+    current_arr = lax.psum(1, "cols")
+    d_next = lax.axis_index("cols")
+    kept_arr, current_block = (current_arr, d_next)
+    fresh = block_here.shape[along_dim] // kept_arr
+    tall = list(block_here.shape)
+    tall[along_dim] = fresh
+    val = tall[k_dim]
+    tall[k_dim] = val * kept_arr
+    state_next = jnp.zeros(tall, block_here.dtype)
+    for c in tuple(range(kept_arr)):
+        y = lax.dynamic_slice_in_dim(block_here, (current_block ^ c) * fresh, fresh, axis=along_dim)
+        if c:
+            y = lax.ppermute(y, "cols", tuple(((num, num ^ c) for num in range(kept_arr))))
+        state_next = lax.dynamic_update_slice_in_dim(
+            state_next, y, (current_block ^ c) * val, axis=k_dim
+        )
+    return state_next
+
+
+pack_the_orders = functools.partial(draft_tails, along_dim=1, k_dim=2)
 
 
 def normalize(matrix):
@@ -43,7 +67,7 @@
     bias_tile = tile_bias(pair, pair_proj)
     key_value = jnp.concatenate([key_rows, values], axis=1)
     gathered = lax.all_gather(key_value, ("rows", "cols"), axis=0, tiled=True)
-    bias_own = lax.all_to_all(bias_tile, "cols", split_axis=1, concat_axis=2, tiled=True)
+    bias_own = pack_the_orders(bias_tile)
     key_count = gathered.shape[0]
     key_heads = gathered[:, :features].reshape(key_count, head_count, head_dim)
     value_heads = gathered[:, features:].reshape(key_count, head_count, head_dim)

time: 86.6 us -> 81.5 us (0.941)
  blocking collectives: 46.1 us -> 42.4 us
  matrix products: 14.6 us -> 12 us
  local copies, waits for them, and re-layouts: 0.87 us -> 2.71 us
    all_to_all x1 -> x0, starting transfers between devices: 6.48 us -> none  [shards(): lax.all_to_all(bias_tile, 'cols', split_axis=1, concat_axis=2, tiled=True)]
    ppermute x0 -> x3, starting transfers between devices: none -> 5.64 us  [draft_tails(): lax.ppermute(y, 'cols', tuple(((num, num ^ c) for num in range(kept_arr))))]
    all_gather x1, blocking collectives: 46.1 us -> 42.4 us  [shards(): gathered = lax.all_gather(key_value, ('rows', 'cols'), axis=0, tiled=True)]
    dot_general x4, matrix products: 12.6 us -> 10.1 us  [project(): jnp.einsum('ikc,ch->hik', pair_normed, pair_proj, preferred_element_type=...]
    dynamic_update_slice x0 -> x3, local copies, waits for them, and re-layouts: none -> 1.02 us  [draft_tails(): lax.dynamic_update_slice_in_dim(state_next, y, (current_block ^ c) * val,...]
  transfers between devices with their start and end apart: 1 -> 3, of which waited for: 0 -> 0; matrix products, arithmetic and copies ran while one was open for 3% -> 4% of each run, Pallas kernels for 0% -> 0%
where the time goes in v1:
time: 81.5 us; the launch traced here: 81 us
  blocking collectives  42.4 us (52%)
  other arithmetic  17.7 us (22%)
  matrix products  12 us (15%)
  starting transfers between devices  5.64 us (7%)
  local copies, waits for them, and re-layouts  2.71 us (3%)
    all_gather x1, blocking collectives, shards(): gathered = lax.all_gather(key_value, ('rows', 'cols'), axis=0, tiled=True)  42.4 us
    dot_general x4, matrix products, project(): jnp.einsum('ikc,ch->hik', pair_normed, pair_proj, preferred_element_type=...  10.1 us
    reduce_sum x5, other arithmetic, normalize(): variance = jnp.mean(centered * centered, axis=-1, keepdims=True)  9.52 us
    reduce_sum x5, other arithmetic, normalize(): average = jnp.mean(matrix, axis=-1, keepdims=True)  6.53 us
    ppermute x3, starting transfers between devices, draft_tails(): lax.ppermute(y, 'cols', tuple(((num, num ^ c) for num in range(kept_arr))))  5.64 us
  transfers between devices with their start and end apart: 3, of which 0 were waited for; matrix products, arithmetic and copies ran while one was open for 4% of the time, Pallas kernels for 0%

profile of v1, /device:TPU:0, one launch (start us, length us, event | category | flops | bytes accessed | tf_op | source)
XLA Modules:
  0.0 81.0 jit_solution(13715690555928553561)
XLA Ops:
  0.0 0.0 copy-start
  0.0 26.1 %while.10 = (s32[]{:T(128)}, bf16[4,16,32,128]{3,1,2,0:T(8,128)(2,1)S(1)}, bf16[4,32,128,128]{3,2,1,0:T(8,128)(2,1)}, bf16[128,16]{0,1:T(8,128)(2,1)}, s32[]{:T(128)}) while((s32[]{:T(128)}, bf16[4,16,32,128]{3,1,2,0:T(8,128)(2,1)S(1)}, bf16[4,32,128,128]{3,2,1,0:T(8,128)(2,1)}, bf16[128,16]{0,1:T(8,128)(2,1)}, s32[]{:T(128)}) %tuple.26), condition=%wide.region_6.7_spmd, body=%wide.region_3.6_spmd.sunk | while | flops 22089728 | bytes 3445865 | solution.py:51
  0.0 1.7 %convert_reduce_fusion.3 = f32[32,128]{1,0:T(8,128)S(1)} fusion(bf16[4,32,128,128]{3,2,1,0:T(8,128)(2,1)} %get-tuple-element.81, s32[]{:T(128)S(6)} %copy.23), kind=kLoop, calls=%fused_computation.clone.1 | loop fusion | flops 1044480 | bytes 1064964 | tf_op jit(solution)/shard_map/while/body/eval_jaxpr/reduce_sum | solution.py:33
  1.7 2.3 %fusion.48 = f32[32,128]{1,0:T(8,128)S(1)} fusion(f32[32,128]{1,0:T(8,128)S(1)} %broadcast_multiply_fusion.3, bf16[4,32,128,128]{3,2,1,0:T(8,128)(2,1)} %get-tuple-element.81, s32[]{:T(128)S(6)} %copy.23), kind=kLoop, calls=%fused_computation.5.clone.1 | loop fusion | flops 2093056 | bytes 1081348 | tf_op jit(solution)/shard_map/while/body/eval_jaxpr/reduce_sum | solution.py:35
  4.1 0.0 copy-done.4
  4.1 2.5 %fusion.49 = bf16[4,16,32,128]{3,1,2,0:T(8,128)(2,1)S(1)} fusion(bf16[4,16,32,128]{3,1,2,0:T(8,128)(2,1)S(1)} %get-tuple-element.75, s32[]{:T(128)S(6)} %copy.23, f32[32,128]{1,0:T(8,128)S(1)} %add_rsqrt_fusion.3, f32[32,128]{1,0:T(8,128)S(1)} %broadcast_multiply_fusion.3, bf16[4,32,128,128]{3,2,1,0:T(8,128)(2,1)} %get-tuple-element.81, ...), kind=kOutput, calls=%fused_computation.9.clone.1 | convolution fusion | flops 18939904 | bytes 1217536 | tf_op jit(solution)/shard_map/while/body/eval_jaxpr/ikc,ch->hik/dot_general | solution.py:47
  6.6 0.0 copy-start.4
  6.6 1.6 %convert_reduce_fusion.3 = f32[32,128]{1,0:T(8,128)S(1)} fusion(bf16[4,32,128,128]{3,2,1,0:T(8,128)(2,1)} %get-tuple-element.81, s32[]{:T(128)S(6)} %copy.23), kind=kLoop, calls=%fused_computation.clone.1 | loop fusion | flops 1044480 | bytes 1064964 | tf_op jit(solution)/shard_map/while/body/eval_jaxpr/reduce_sum | solution.py:33
  8.2 2.3 %fusion.48 = f32[32,128]{1,0:T(8,128)S(1)} fusion(f32[32,128]{1,0:T(8,128)S(1)} %broadcast_multiply_fusion.3, bf16[4,32,128,128]{3,2,1,0:T(8,128)(2,1)} %get-tuple-element.81, s32[]{:T(128)S(6)} %copy.23), kind=kLoop, calls=%fused_computation.5.clone.1 | loop fusion | flops 2093056 | bytes 1081348 | tf_op jit(solution)/shard_map/while/body/eval_jaxpr/reduce_sum | solution.py:35
  10.6 2.5 %fusion.49 = bf16[4,16,32,128]{3,1,2,0:T(8,128)(2,1)S(1)} fusion(bf16[4,16,32,128]{3,1,2,0:T(8,128)(2,1)S(1)} %get-tuple-element.75, s32[]{:T(128)S(6)} %copy.23, f32[32,128]{1,0:T(8,128)S(1)} %add_rsqrt_fusion.3, f32[32,128]{1,0:T(8,128)S(1)} %broadcast_multiply_fusion.3, bf16[4,32,128,128]{3,2,1,0:T(8,128)(2,1)} %get-tuple-element.81, ...), kind=kOutput, calls=%fused_computation.9.clone.1 | convolution fusion | flops 18939904 | bytes 1217536 | tf_op jit(solution)/shard_map/while/body/eval_jaxpr/ikc,ch->hik/dot_general | solution.py:47
  13.1 0.0 copy-start.4
  13.1 1.6 %convert_reduce_fusion.3 = f32[32,128]{1,0:T(8,128)S(1)} fusion(bf16[4,32,128,128]{3,2,1,0:T(8,128)(2,1)} %get-tuple-element.81, s32[]{:T(128)S(6)} %copy.23), kind=kLoop, calls=%fused_computation.clone.1 | loop fusion | flops 1044480 | bytes 1064964 | tf_op jit(solution)/shard_map/while/body/eval_jaxpr/reduce_sum | solution.py:33
  14.7 2.3 %fusion.48 = f32[32,128]{1,0:T(8,128)S(1)} fusion(f32[32,128]{1,0:T(8,128)S(1)} %broadcast_multiply_fusion.3, bf16[4,32,128,128]{3,2,1,0:T(8,128)(2,1)} %get-tuple-element.81, s32[]{:T(128)S(6)} %copy.23), kind=kLoop, calls=%fused_computation.5.clone.1 | loop fusion | flops 2093056 | bytes 1081348 | tf_op jit(solution)/shard_map/while/body/eval_jaxpr/reduce_sum | solution.py:35
  17.1 0.0 copy-done.4
  17.1 2.5 %fusion.49 = bf16[4,16,32,128]{3,1,2,0:T(8,128)(2,1)S(1)} fusion(bf16[4,16,32,128]{3,1,2,0:T(8,128)(2,1)S(1)} %get-tuple-element.75, s32[]{:T(128)S(6)} %copy.23, f32[32,128]{1,0:T(8,128)S(1)} %add_rsqrt_fusion.3, f32[32,128]{1,0:T(8,128)S(1)} %broadcast_multiply_fusion.3, bf16[4,32,128,128]{3,2,1,0:T(8,128)(2,1)} %get-tuple-element.81, ...), kind=kOutput, calls=%fused_computation.9.clone.1 | convolution fusion | flops 18939904 | bytes 1217536 | tf_op jit(solution)/shard_map/while/body/eval_jaxpr/ikc,ch->hik/dot_general | solution.py:47
  19.6 0.0 copy-start.4
  19.7 1.6 %convert_reduce_fusion.3 = f32[32,128]{1,0:T(8,128)S(1)} fusion(bf16[4,32,128,128]{3,2,1,0:T(8,128)(2,1)} %get-tuple-element.81, s32[]{:T(128)S(6)} %copy.23), kind=kLoop, calls=%fused_computation.clone.1 | loop fusion | flops 1044480 | bytes 1064964 | tf_op jit(solution)/shard_map/while/body/eval_jaxpr/reduce_sum | solution.py:33
  21.2 2.3 %fusion.48 = f32[32,128]{1,0:T(8,128)S(1)} fusion(f32[32,128]{1,0:T(8,128)S(1)} %broadcast_multiply_fusion.3, bf16[4,32,128,128]{3,2,1,0:T(8,128)(2,1)} %get-tuple-element.81, s32[]{:T(128)S(6)} %copy.23), kind=kLoop, calls=%fused_computation.5.clone.1 | loop fusion | flops 2093056 | bytes 1081348 | tf_op jit(solution)/shard_map/while/body/eval_jaxpr/reduce_sum | solution.py:35
  23.6 2.5 %fusion.49 = bf16[4,16,32,128]{3,1,2,0:T(8,128)(2,1)S(1)} fusion(bf16[4,16,32,128]{3,1,2,0:T(8,128)(2,1)S(1)} %get-tuple-element.75, s32[]{:T(128)S(6)} %copy.23, f32[32,128]{1,0:T(8,128)S(1)} %add_rsqrt_fusion.3, f32[32,128]{1,0:T(8,128)S(1)} %broadcast_multiply_fusion.3, bf16[4,32,128,128]{3,2,1,0:T(8,128)(2,1)} %get-tuple-element.81, ...), kind=kOutput, calls=%fused_computation.9.clone.1 | convolution fusion | flops 18939904 | bytes 1217536 | tf_op jit(solution)/shard_map/while/body/eval_jaxpr/ikc,ch->hik/dot_general | solution.py:47
  26.1 0.0 copy-start.2
  26.2 0.0 copy-start.3
  26.2 0.1 copy.16
  26.4 0.8 constant_dynamic-slice_fusion
  27.2 5.1 %collective-permute-start.2 = (bf16[16,32,128]{2,1,0:T(8,128)(2,1)}, bf16[16,32,128]{2,1,0:T(8,128)(2,1)S(1)}, u32[]{:S(2)}, u32[]{:S(2)}) collective-permute-start(bf16[16,32,128]{2,1,0:T(8,128)(2,1)} %get-tuple-element.38), channel_id=1, source_target_pairs={{0,3},{1,2},{2,1},{3,0},{4,7},{5,6},{6,5},{7,4},{8,11},{9,10},{10,... | collective-permute-start | bytes 393224 | tf_op jit(solution)/shard_map/ppermute | solution.py:22
  32.2 0.0 collective-permute-start.1
  32.2 0.6 collective-permute-start
  32.8 0.0 copy-done.2
  32.8 0.1 convert_reduce_fusion.1
  32.9 0.2 fusion.20
  33.1 0.0 copy-done
  33.1 0.4 fusion.29
  33.5 42.4 %all_gather.3 = bf16[512,768]{1,0:T(8,128)(2,1)S(1)} all-gather(bf16[32,768]{1,0:T(8,128)(2,1)S(1)} %slice.53), channel_id=1, replica_groups=mesh['parts'=2,'rows'=4,'cols'=4] {'rows','cols'}, dimensions={0}, use_global_device_ids=true | all-gather | bytes 835584 | tf_op jit(solution)/shard_map/all_gather | solution.py:69
  76.0 0.1 fusion.35
  76.0 0.6 slice_reduce_fusion
  76.7 0.6 iota_compare_fusion
  77.4 0.1 copy.18
  77.5 0.2 copy.14
  77.7 0.2 copy.13
  77.9 0.0 collective-permute-done
  77.9 0.9 %constant_dynamic-update-slice_fusion.1 = bf16[16,32,512]{2,1,0:T(8,128)(2,1)S(1)} fusion(bf16[16,32,512]{2,1,0:T(8,128)(2,1)S(1)} %get-tuple-element.41, bf16[16,32,128]{2,1,0:T(8,128)(2,1)} %collective-permute-done, s32[]{:T(128)S(6)} %select_n.31), kind=kLoop, calls=%fused_computation.49 | loop fusion | bytes 262148 | tf_op jit(solution)/shard_map/dynamic_update_slice | solution.py:23
  78.8 0.0 collective-permute-done.1
  78.9 0.0 collective-permute-done.2
  79.0 0.0 copy-start.1
  79.0 0.5 fusion.36
  79.4 0.3 fusion.14
  79.8 0.3 fusion.13
  80.1 0.1 copy.19
  80.2 0.8 convolution_convert_fusion.1
  (23 shorter events, 0.2 us)
Async XLA Ops:
  0.0 33.1 %copy-start = (bf16[384,1536]{1,0:T(8,128)(2,1)S(1)}, bf16[384,1536]{1,0:T(8,128)(2,1)}, u32[]{:S(2)}) copy-start(bf16[384,1536]{1,0:T(8,128)(2,1)} %param.12) | copy-start | bytes 3538948
  0.0 4.1 %copy-start.4 = (bf16[128,16]{0,1:T(8,128)(2,1)S(1)}, bf16[128,16]{0,1:T(8,128)(2,1)}, u32[]{:S(2)}) copy-start(bf16[128,16]{0,1:T(8,128)(2,1)} %get-tuple-element.82) | copy-start | bytes 12292 | tf_op jit(solution)/shard_map/while
  6.6 4.0 %copy-start.4 = (bf16[128,16]{0,1:T(8,128)(2,1)S(1)}, bf16[128,16]{0,1:T(8,128)(2,1)}, u32[]{:S(2)}) copy-start(bf16[128,16]{0,1:T(8,128)(2,1)} %get-tuple-element.82) | copy-start | bytes 12292 | tf_op jit(solution)/shard_map/while
  13.1 4.0 %copy-start.4 = (bf16[128,16]{0,1:T(8,128)(2,1)S(1)}, bf16[128,16]{0,1:T(8,128)(2,1)}, u32[]{:S(2)}) copy-start(bf16[128,16]{0,1:T(8,128)(2,1)} %get-tuple-element.82) | copy-start | bytes 12292 | tf_op jit(solution)/shard_map/while
  19.6 4.0 %copy-start.4 = (bf16[128,16]{0,1:T(8,128)(2,1)S(1)}, bf16[128,16]{0,1:T(8,128)(2,1)}, u32[]{:S(2)}) copy-start(bf16[128,16]{0,1:T(8,128)(2,1)} %get-tuple-element.82) | copy-start | bytes 12292 | tf_op jit(solution)/shard_map/while
  26.1 6.7 %copy-start.2 = (bf16[32,384]{1,0:T(8,128)(2,1)S(1)}, bf16[32,384]{1,0:T(8,128)(2,1)}, u32[]{:S(2)}) copy-start(bf16[32,384]{1,0:T(8,128)(2,1)} %param.9) | copy-start | bytes 73732
  26.2 7.3 %copy-start.3 = (f32[384]{0:T(512)S(1)}, f32[384]{0:T(512)}, u32[]{:S(2)}) copy-start(f32[384]{0:T(512)} %param.13) | copy-start | bytes 4612
  27.2 48.9 %copy-start.5 = (s32[8]{0:T(128)S(1)}, s32[8]{0:T(128)}, u32[]{:S(2)}) copy-start(s32[8]{0:T(128)} %param.11) | copy-start | bytes 100
  27.2 51.7 %collective-permute-start.2 = (bf16[16,32,128]{2,1,0:T(8,128)(2,1)}, bf16[16,32,128]{2,1,0:T(8,128)(2,1)S(1)}, u32[]{:S(2)}, u32[]{:S(2)}) collective-permute-start(bf16[16,32,128]{2,1,0:T(8,128)(2,1)} %get-tuple-element.38), channel_id=1, source_target_pairs={{0,3},{1,2},{2,1},{3,0},{4,7},{5,6},{6,5},{7,4},{8,11},{9,10},{10,... | collective-permute-start | bytes 393224 | tf_op jit(solution)/shard_map/ppermute | solution.py:22
  32.2 46.6 %collective-permute-start.1 = (bf16[16,32,128]{2,1,0:T(8,128)(2,1)}, bf16[16,32,128]{2,1,0:T(8,128)(2,1)S(1)}, u32[]{:S(2)}, u32[]{:S(2)}) collective-permute-start(bf16[16,32,128]{2,1,0:T(8,128)(2,1)} %get-tuple-element.39), channel_id=1, source_target_pairs={{0,2},{1,3},{2,0},{3,1},{4,6},{5,7},{6,4},{7,5},{8,10},{9,11},{10,... | collective-permute-start | bytes 393224 | tf_op jit(solution)/shard_map/ppermute | solution.py:22
  32.2 45.7 %collective-permute-start = (bf16[16,32,128]{2,1,0:T(8,128)(2,1)}, bf16[16,32,128]{2,1,0:T(8,128)(2,1)}, u32[]{:S(2)}, u32[]{:S(2)}) collective-permute-start(bf16[16,32,128]{2,1,0:T(8,128)(2,1)} %get-tuple-element.40), channel_id=1, source_target_pairs={{0,1},{1,0},{2,3},{3,2},{4,5},{5,4},{6,7},{7,6},{8,9},{9,8},{10,11... | collective-permute-start | bytes 393224 | tf_op jit(solution)/shard_map/ppermute | solution.py:22
  79.0 1.3 %copy-start.1 = (bf16[384,384]{1,0:T(8,128)(2,1)S(1)}, bf16[384,384]{1,0:T(8,128)(2,1)}, u32[]{:S(2)}) copy-start(bf16[384,384]{1,0:T(8,128)(2,1)} %param.15) | copy-start | bytes 884740
